TPU v7x, 32 devices: a whole 2x2x4 slice. The times are simulated.
32 devices in a mesh: gx: 4 (over z), gy: 4 (over y, x), gz: 2 (over core).
Axes of the slice: x: 2, y: 2, z: 4, core: 2. Of those that a mesh axis runs over, the one named last changes fastest.
Arguments:
- schur: bfloat16 [4, 4, 2, 2048, 2048], P('gx', 'gy', 'gz'), may hold values from -0.09375 to 0.09375
- interface_diag: float32 [4, 4, 2, 2048], P('gx', 'gy', 'gz'), may hold values from 2 to 4
- precond: float32 [4, 4, 2, 16, 128, 128], P('gx', 'gy', 'gz'), may hold values from -0.3 to 0.8
- load: bfloat16 [4, 4, 2, 2048, 256], P('gx', 'gy', 'gz'), may hold values from -170 to 170
- face_blocks: int32 [4, 4, 2, 6, 2], P('gx', 'gy', 'gz'), may hold values from 0 to 16, as said below
Outputs:
- solution: float32 [4, 4, 2, 2048, 256], P('gx', 'gy', 'gz')
- residual_norm: float32 [256], replicated
Inputs may be any that keep to these rules, and one draw needn't show every extreme that they name: `face_blocks`: for each subdomain p and direction d (0, 1: next and previous along the first grid dimension; 2, 3 and 4, 5 likewise along the second and third), slots 0 to n - 1 hold block numbers below 16 shared with the neighbour in that direction, where n (1 to 2 inside the grid, 0 across its boundary) equals the neighbour's n for the opposite direction, and the neighbour's slot k of the opposite direction holds the block that shares with p's slot k; the remaining slots hold 16; no block number appears twice in one subdomain's table; some face shares 2 blocks in every draw.
All inputs are finite; a program needn't handle non-finite values.
Results may differ from a plain program's by a relative error of at most 0.0008.
Values sent between devices are 32-bit elements; how exact they have to be, the bound alone decides.
A program may use at most 128 MiB of HBM per device.

v0:
```python
import jax
import jax.numpy as jnp
from jax import lax
from jax.sharding import PartitionSpec as P

epsilon = 1e-06


def extended_2(value, sides, width):
    for axis, dim in sides:
        peers, length = (lax.axis_size(axis), value.shape[dim])
        up = [(i, (i + 1) % peers) for i in range(peers - 1)]
        down = [(j, i) for i, j in up]
        last = lax.slice_in_dim(value, length - width, length, axis=dim)
        leading = lax.slice_in_dim(value, 0, width, axis=dim)
        before = lax.ppermute(last, axis, up)
        after = lax.ppermute(leading, axis, down)
        value = jnp.concatenate([before, value, after], axis=dim)
    return value


def assemble(blocks, slot_index, live_mask):
    block_count, block_rows, row_width = blocks.shape
    slot_count = slot_index.shape[1]
    extended = jnp.concatenate([blocks, jnp.zeros((1, block_rows, row_width), jnp.float32)], axis=0)
    slot_flat = slot_index.reshape(-1)
    packed = extended[slot_flat].reshape(6, slot_count, block_rows, row_width)
    gx_faces = extended_2(jnp.stack([packed[1], packed[0]], 0), (("gx", 0),), 1)
    gy_faces = extended_2(jnp.stack([packed[3], packed[2]], 0), (("gy", 0),), 1)
    gz_faces = extended_2(jnp.stack([packed[5], packed[4]], 0), (("gz", 0),), 1)
    arrived = jnp.stack(
        [gx_faces[3], gx_faces[0], gy_faces[3], gy_faces[0], gz_faces[3], gz_faces[0]], 0
    )
    extended = extended.at[slot_flat].add(arrived.reshape(6 * slot_count, block_rows, row_width))
    return extended[:block_count] * live_mask[:, None, None]


def partial_product(left_vec, right_vec):
    return 0.5 * jnp.sum(left_vec * right_vec, axis=(0, 1))


def on_device(schur, interface_diag, precond, load, face_blocks):
    block_count = precond.shape[3]
    block_rows = precond.shape[4]
    rhs_count = load.shape[-1]
    slot_index = face_blocks.reshape(6, face_blocks.shape[-1])
    slot_hits = slot_index[:, :, None] == jnp.arange(block_count, dtype=jnp.int32)
    live_mask = jnp.any(slot_hits, axis=(0, 1)).astype(jnp.float32)
    matrix = schur.reshape(schur.shape[-2], schur.shape[-1])
    diag_column = interface_diag.reshape(-1, 1)
    local_blocks = precond.reshape(block_count, block_rows, block_rows)
    assembled_load = assemble(
        load.reshape(block_count, block_rows, rhs_count).astype(jnp.float32), slot_index, live_mask
    )

    def precondition(vector):
        partial_value = jnp.einsum(
            "bij,bjr->bir", local_blocks, vector, precision=lax.Precision.HIGHEST
        )
        return assemble(partial_value, slot_index, live_mask)

    def operate(vector):
        flattened = vector.reshape(block_count * block_rows, rhs_count)
        narrow = flattened.astype(jnp.bfloat16)
        product = jnp.dot(matrix, narrow, preferred_element_type=jnp.float32)
        partial_value = product + diag_column * flattened
        return assemble(
            partial_value.reshape(block_count, block_rows, rhs_count), slot_index, live_mask
        )

    precond_raw = precondition(assembled_load)
    working_raw = operate(precond_raw)
    load_square, cross_first, raw_square = lax.psum(
        (
            partial_product(assembled_load, assembled_load),
            partial_product(working_raw, assembled_load),
            partial_product(working_raw, working_raw),
        ),
        ("gx", "gy", "gz"),
    )
    initial = jnp.sqrt(load_square + epsilon)
    rescale = 1.0 / initial
    basis_first = assembled_load * rescale
    precond_first = precond_raw * rescale
    diag_first = cross_first * rescale * rescale
    working = working_raw * rescale - diag_first * basis_first
    below_first = jnp.sqrt(
        jnp.maximum(raw_square * rescale * rescale - diag_first * diag_first, 0.0) + epsilon
    )
    basis_second = working / below_first
    precond_second = precondition(basis_second)
    working = operate(precond_second)
    upper_second, diag_second, work_square = lax.psum(
        (
            partial_product(working, basis_first),
            partial_product(working, basis_second),
            partial_product(working, working),
        ),
        ("gx", "gy", "gz"),
    )
    below_second = jnp.sqrt(
        jnp.maximum(work_square - upper_second * upper_second - diag_second * diag_second, 0.0)
        + epsilon
    )
    radius_first = jnp.sqrt(diag_first * diag_first + below_first * below_first)
    cosine_first = diag_first / radius_first
    sine_first = below_first / radius_first
    rotated_top = cosine_first * upper_second + sine_first * diag_second
    rotated_low = cosine_first * diag_second - sine_first * upper_second
    radius_second = jnp.sqrt(rotated_low * rotated_low + below_second * below_second)
    cosine_second = rotated_low / radius_second
    sine_second = below_second / radius_second
    weight_second = -initial * sine_first * cosine_second / radius_second
    weight_first = (initial * cosine_first - rotated_top * weight_second) / radius_first
    solution = weight_first * precond_first + weight_second * precond_second
    residual_norm = initial * sine_first * sine_second
    return (solution.reshape(1, 1, 1, block_count * block_rows, rhs_count), residual_norm)


def solution(mesh):
    placed = (
        P("gx", "gy", "gz", None, None),
        P("gx", "gy", "gz", None),
        P("gx", "gy", "gz", None, None, None),
        P("gx", "gy", "gz", None, None),
        P("gx", "gy", "gz", None, None),
    )
    return jax.shard_map(
        on_device,
        mesh=mesh,
        in_specs=placed,
        out_specs=(P("gx", "gy", "gz", None, None), P()),
        check_vma=False,
    )
```

profile of v0, /device:TPU:0, one launch (start us, length us, event | category | flops | bytes accessed | tf_op | source)
XLA Modules:
  0.0 332.8 jit_solution(5682009236857555295)
XLA Ops:
  3.1 1.8 gather_fusion
  7.7 5.6 %collective-permute-start.1 = (f32[1,2,128,256]{3,2,1,0:T(8,128)S(1)}, f32[1,2,128,256]{3,2,1,0:T(8,128)S(1)}, u32[]{:S(2)}, u32[]{:S(2)}) collective-permute-start(f32[1,2,128,256]{3,2,1,0:T(8,128)S(1)} %get-tuple-element.51), channel_id=1, source_target_pairs={{0,8},{8,16},{16,24},{1,9},{9,17},{17,25},{2,10},{10,18},{18,26},{... | collective-permute-start | bytes 786440 | tf_op jit(solution)/shard_map/ppermute | solution.py:16
  17.6 4.4 %collective-permute-start.3 = (f32[1,2,128,256]{3,2,1,0:T(8,128)S(1)}, f32[1,2,128,256]{3,2,1,0:T(8,128)S(1)}, u32[]{:S(2)}, u32[]{:S(2)}) collective-permute-start(f32[1,2,128,256]{3,2,1,0:T(8,128)S(1)} %get-tuple-element.49), channel_id=1, source_target_pairs={{0,2},{2,4},{4,6},{1,3},{3,5},{5,7},{8,10},{10,12},{12,14},{9,11},... | collective-permute-start | bytes 786440 | tf_op jit(solution)/shard_map/ppermute | solution.py:16
  22.1 4.8 %collective-permute-done.2 = f32[1,2,128,256]{3,2,1,0:T(8,128)S(1)} collective-permute-done((f32[1,2,128,256]{3,2,1,0:T(8,128)S(1)}, f32[1,2,128,256]{3,2,1,0:T(8,128)S(1)}, u32[]{:S(2)}, u32[]{:S(2)}) %collective-permute-start.2) | collective-permute-done | bytes 262176 | tf_op jit(solution)/shard_map/ppermute | solution.py:17
  29.9 3.1 scatter_fusion
  33.0 3.8 %convolution_bitcast_fusion.1 = f32[16,128,256]{1,2,0:T(8,128)S(1)} fusion(f32[17,128,256]{2,1,0:T(8,128)S(1)} %scatter_fusion, f32[1,1,1,16,128,128]{5,4,3,2,1,0:T(8,128)S(1)} %copy-done, f32[16]{0:T(128)S(1)} %convert_element_type.24), kind=kOutput, calls=%fused_computation.32 | convolution fusion | flops 805830656 | bytes 5243392 | tf_op jit(solution)/shard_map/bij,bjr->bir/dot_general | solution.py:57
  38.5 3.4 %gather_fusion.1 = f32[12,128,256]{1,2,0:T(8,128)} fusion(f32[17,128,256]{1,2,0:T(8,128)} %concatenate.19, s32[1024]{0:T(1024)S(1)} %pad_clamp_fusion), kind=kCustom, calls=%fused_computation.1 | custom fusion | bytes 3145776 | tf_op jit(solution)/shard_map/gather | solution.py:27
  41.9 2.5 slice_bitcast_fusion.18
  45.6 5.3 %collective-permute-start.7 = (f32[1,2,128,256]{2,3,1,0:T(8,128)}, f32[1,2,128,256]{2,3,1,0:T(8,128)}, u32[]{:S(2)}, u32[]{:S(2)}) collective-permute-start(f32[1,2,128,256]{2,3,1,0:T(8,128)} %get-tuple-element.45), channel_id=1, source_target_pairs={{0,8},{8,16},{16,24},{1,9},{9,17},{17,25},{2,10},{10,18},{18,26},{... | collective-permute-start | bytes 786440 | tf_op jit(solution)/shard_map/ppermute | solution.py:16
  52.2 3.0 copy.23
  57.9 6.6 %collective-permute-start.9 = (f32[1,2,128,256]{2,3,1,0:T(8,128)}, f32[1,2,128,256]{2,3,1,0:T(8,128)S(1)}, u32[]{:S(2)}, u32[]{:S(2)}) collective-permute-start(f32[1,2,128,256]{2,3,1,0:T(8,128)} %get-tuple-element.43), channel_id=1, source_target_pairs={{0,2},{2,4},{4,6},{1,3},{3,5},{5,7},{8,10},{10,12},{12,14},{9,11},... | collective-permute-start | bytes 786440 | tf_op jit(solution)/shard_map/ppermute | solution.py:16
  73.3 3.0 copy.24
  76.3 4.5 %scatter_fusion.1 = f32[17,128,256]{2,1,0:T(8,128)} fusion(f32[17,128,256]{2,1,0:T(8,128)} %copy.23, s32[12]{0:T(128)S(1)} %fusion.24, f32[12,128,256]{2,1,0:T(8,128)} %copy.24), kind=kCustom, calls=%fused_computation.6 | custom fusion | flops 393216 | bytes 4718640 | tf_op jit(solution)/shard_map/scatter-add | solution.py:34
  80.8 3.6 %fusion.28 = (bf16[16,128,256]{2,1,0:T(8,128)(2,1)}, f32[16,128,256]{2,1,0:T(8,128)}) fusion(f32[16]{0:T(128)S(1)} %convert_element_type.24, f32[17,128,256]{2,1,0:T(8,128)} %scatter_fusion.1), kind=kLoop, calls=%fused_computation.126 | loop fusion | flops 1048576 | bytes 5242944 | tf_op jit(solution)/shard_map/convert_element_type | solution.py:64
  84.4 2.9 copy.25
  87.3 8.0 %fusion.13 = f32[2048,256]{0,1:T(8,128)} fusion(bf16[2048,256]{1,0:T(8,128)(2,1)} %bitcast.116, bf16[1,1,1,2048,2048]{4,3,2,1,0:T(8,128)(2,1)} %param.5, f32[2048,256]{0,1:T(8,128)} %copy.25, f32[2048]{0:T(1024)S(1)} %bitcast.119), kind=kOutput, calls=%fused_computation.17 | convolution fusion | flops 2148532224 | bytes 13639680 | tf_op jit(solution)/shard_map/dot_general | solution.py:65
  95.3 2.9 copy.26
  98.2 3.2 concatenate.20
  101.4 3.4 %gather_fusion.2 = f32[12,128,256]{2,1,0:T(8,128)} fusion(f32[17,128,256]{2,1,0:T(8,128)} %concatenate.20, s32[1024]{0:T(1024)S(1)} %pad_clamp_fusion), kind=kCustom, calls=%fused_computation.2 | custom fusion | bytes 3145776 | tf_op jit(solution)/shard_map/gather | solution.py:27
  107.7 4.6 %collective-permute-start.13 = (f32[1,2,128,256]{3,2,1,0:T(8,128)S(1)}, f32[1,2,128,256]{3,2,1,0:T(8,128)S(1)}, u32[]{:S(2)}, u32[]{:S(2)}) collective-permute-start(f32[1,2,128,256]{3,2,1,0:T(8,128)S(1)} %get-tuple-element.39), channel_id=1, source_target_pairs={{0,8},{8,16},{16,24},{1,9},{9,17},{17,25},{2,10},{10,18},{18,26},{... | collective-permute-start | bytes 786440 | tf_op jit(solution)/shard_map/ppermute | solution.py:16
  116.7 5.5 %collective-permute-start.15 = (f32[1,2,128,256]{3,2,1,0:T(8,128)S(1)}, f32[1,2,128,256]{3,2,1,0:T(8,128)S(1)}, u32[]{:S(2)}, u32[]{:S(2)}) collective-permute-start(f32[1,2,128,256]{3,2,1,0:T(8,128)S(1)} %get-tuple-element.37), channel_id=1, source_target_pairs={{0,2},{2,4},{4,6},{1,3},{3,5},{5,7},{8,10},{10,12},{12,14},{9,11},... | collective-permute-start | bytes 786440 | tf_op jit(solution)/shard_map/ppermute | solution.py:16
  124.4 4.3 %collective-permute-done.15 = f32[1,2,128,256]{3,2,1,0:T(8,128)S(1)} collective-permute-done((f32[1,2,128,256]{3,2,1,0:T(8,128)S(1)}, f32[1,2,128,256]{3,2,1,0:T(8,128)S(1)}, u32[]{:S(2)}, u32[]{:S(2)}) %collective-permute-start.15) | collective-permute-done | bytes 262176 | tf_op jit(solution)/shard_map/ppermute | solution.py:16
  130.9 4.5 %scatter_fusion.2 = f32[17,128,256]{2,1,0:T(8,128)} fusion(f32[17,128,256]{2,1,0:T(8,128)} %concatenate.20, s32[12]{0:T(128)S(1)} %fusion.24, f32[12,128,256]{2,1,0:T(8,128)} %bitcast.31), kind=kCustom, calls=%fused_computation.7 | custom fusion | flops 393216 | bytes 4718640 | tf_op jit(solution)/shard_map/scatter-add | solution.py:34
  135.5 2.2 multiply_reduce_fusion.4
  137.7 44.0 %all-reduce.6 = (f32[256]{0:T(256)S(1)}, f32[256]{0:T(256)S(1)}, f32[256]{0:T(256)S(1)}) all-reduce(f32[256]{0:T(256)S(1)} %broadcast_multiply_fusion.5, f32[256]{0:T(256)S(1)} %get-tuple-element.54, f32[256]{0:T(256)S(1)} %get-tuple-element.55), channel_id=1, replica_groups=mesh['gx'=4,'gy'=4,'gz'=2] {'gx','gy','gz'}, use_global_device_ids=true, to_apply=%region_3.0 | all-reduce | flops 768 | bytes 6144 | tf_op jit(solution)/shard_map/psum | solution.py:73
  181.7 5.7 %convolution_bitcast_fusion = f32[16,128,256]{1,2,0:T(8,128)S(1)} fusion(f32[1,1,1,16,128,128]{5,4,3,2,1,0:T(8,128)S(1)} %copy-done, f32[17,128,256]{2,1,0:T(8,128)} %scatter_fusion.2, f32[17,128,256]{2,1,0:T(8,128)S(1)} %scatter_fusion, f32[256]{0:T(256)S(1)} %get-tuple-element.18, f32[256]{0:T(256)S(1)} %get-tuple-element.19, ...), kind=kOutput, calls=%fused_computation.31 | convolution fusion | flops 808976384 | bytes 7343616 | tf_op jit(solution)/shard_map/bij,bjr->bir/dot_general | solution.py:57
  189.1 3.4 %gather_fusion.3 = f32[12,128,256]{1,2,0:T(8,128)} fusion(f32[17,128,256]{1,2,0:T(8,128)} %concatenate.21, s32[1024]{0:T(1024)S(1)} %pad_clamp_fusion), kind=kCustom, calls=%fused_computation.3 | custom fusion | bytes 3145776 | tf_op jit(solution)/shard_map/gather | solution.py:27
  192.5 2.1 slice_bitcast_fusion.6
  195.9 5.3 %collective-permute-start.19 = (f32[1,2,128,256]{2,3,1,0:T(8,128)S(1)}, f32[1,2,128,256]{2,3,1,0:T(8,128)}, u32[]{:S(2)}, u32[]{:S(2)}) collective-permute-start(f32[1,2,128,256]{2,3,1,0:T(8,128)S(1)} %get-tuple-element.33), channel_id=1, source_target_pairs={{0,8},{8,16},{16,24},{1,9},{9,17},{17,25},{2,10},{10,18},{18,26},{... | collective-permute-start | bytes 786440 | tf_op jit(solution)/shard_map/ppermute | solution.py:16
  202.5 3.0 copy.28
  208.1 4.8 %collective-permute-start.21 = (f32[1,2,128,256]{2,3,1,0:T(8,128)S(1)}, f32[1,2,128,256]{2,3,1,0:T(8,128)S(1)}, u32[]{:S(2)}, u32[]{:S(2)}) collective-permute-start(f32[1,2,128,256]{2,3,1,0:T(8,128)S(1)} %get-tuple-element.31), channel_id=1, source_target_pairs={{0,2},{2,4},{4,6},{1,3},{3,5},{5,7},{8,10},{10,12},{12,14},{9,11},... | collective-permute-start | bytes 786440 | tf_op jit(solution)/shard_map/ppermute | solution.py:16
  213.0 1.7 constant_dynamic-update-slice_fusion.23
  214.6 1.7 constant_dynamic-update-slice_fusion.22
  221.7 3.0 copy.29
  224.7 4.5 %scatter_fusion.3 = f32[17,128,256]{2,1,0:T(8,128)} fusion(f32[17,128,256]{2,1,0:T(8,128)} %copy.28, s32[12]{0:T(128)S(1)} %fusion.24, f32[12,128,256]{2,1,0:T(8,128)} %copy.29), kind=kCustom, calls=%fused_computation.8 | custom fusion | flops 393216 | bytes 4718640 | tf_op jit(solution)/shard_map/scatter-add | solution.py:34
  229.2 3.3 fusion.27
  232.5 2.9 copy.30
  235.4 7.7 %fusion.10 = f32[2048,256]{0,1:T(8,128)} fusion(bf16[2048,256]{1,0:T(8,128)(2,1)S(1)} %bitcast.117, bf16[1,1,1,2048,2048]{4,3,2,1,0:T(8,128)(2,1)} %param.5, f32[2048,256]{0,1:T(8,128)} %copy.30, f32[2048]{0:T(1024)S(1)} %bitcast.120), kind=kOutput, calls=%fused_computation.16 | convolution fusion | flops 2148532224 | bytes 13639680 | tf_op jit(solution)/shard_map/dot_general | solution.py:65
  243.1 3.0 copy.31
  246.1 3.2 concatenate.22
  249.3 3.4 %gather_fusion.4 = f32[12,128,256]{2,1,0:T(8,128)} fusion(f32[17,128,256]{2,1,0:T(8,128)} %concatenate.22, s32[1024]{0:T(1024)S(1)} %pad_clamp_fusion), kind=kCustom, calls=%fused_computation.4 | custom fusion | bytes 3145776 | tf_op jit(solution)/shard_map/gather | solution.py:27
  255.5 4.6 %collective-permute-start.25 = (f32[1,2,128,256]{3,2,1,0:T(8,128)S(1)}, f32[1,2,128,256]{3,2,1,0:T(8,128)S(1)}, u32[]{:S(2)}, u32[]{:S(2)}) collective-permute-start(f32[1,2,128,256]{3,2,1,0:T(8,128)S(1)} %get-tuple-element.27), channel_id=1, source_target_pairs={{0,8},{8,16},{16,24},{1,9},{9,17},{17,25},{2,10},{10,18},{18,26},{... | collective-permute-start | bytes 786440 | tf_op jit(solution)/shard_map/ppermute | solution.py:16
  264.5 5.5 %collective-permute-start.27 = (f32[1,2,128,256]{3,2,1,0:T(8,128)S(1)}, f32[1,2,128,256]{3,2,1,0:T(8,128)S(1)}, u32[]{:S(2)}, u32[]{:S(2)}) collective-permute-start(f32[1,2,128,256]{3,2,1,0:T(8,128)S(1)} %get-tuple-element.25), channel_id=1, source_target_pairs={{0,2},{2,4},{4,6},{1,3},{3,5},{5,7},{8,10},{10,12},{12,14},{9,11},... | collective-permute-start | bytes 786440 | tf_op jit(solution)/shard_map/ppermute | solution.py:16
  272.2 4.0 %collective-permute-done.27 = f32[1,2,128,256]{3,2,1,0:T(8,128)S(1)} collective-permute-done((f32[1,2,128,256]{3,2,1,0:T(8,128)S(1)}, f32[1,2,128,256]{3,2,1,0:T(8,128)S(1)}, u32[]{:S(2)}, u32[]{:S(2)}) %collective-permute-start.27) | collective-permute-done | bytes 262176 | tf_op jit(solution)/shard_map/ppermute | solution.py:16
  278.5 4.5 %scatter_fusion.4 = f32[17,128,256]{2,1,0:T(8,128)} fusion(f32[17,128,256]{2,1,0:T(8,128)} %concatenate.22, s32[12]{0:T(128)S(1)} %fusion.24, f32[12,128,256]{2,1,0:T(8,128)} %bitcast.50), kind=kCustom, calls=%fused_computation.9 | custom fusion | flops 393216 | bytes 4718640 | tf_op jit(solution)/shard_map/scatter-add | solution.py:34
  282.9 3.2 multiply_reduce_fusion.2
  286.2 42.0 %all-reduce.5 = (f32[256]{0:T(256)S(1)}, f32[256]{0:T(256)S(1)}, f32[256]{0:T(256)S(1)}) all-reduce(f32[256]{0:T(256)S(1)} %broadcast_multiply_fusion.1, f32[256]{0:T(256)S(1)} %broadcast_multiply_fusion, f32[256]{0:T(256)S(1)} %broadcast_multiply_fusion.2), channel_id=1, replica_groups=mesh['gx'=4,'gy'=4,'gz'=2] {'gx','gy','gz'}, use_global_device_ids=true, to_apply=%region_15.0 | all-reduce | flops 768 | bytes 6144 | tf_op jit(solution)/shard_map/psum | solution.py:93
  328.9 4.0 %multiply_add_fusion = f32[16,128,256]{2,1,0:T(8,128)} fusion(f32[16,128,256]{2,1,0:T(8,128)} %get-tuple-element.17, f32[16,128,256]{2,1,0:T(8,128)} %get-tuple-element.22, f32[256]{0:T(256)S(1)} %get-tuple-element.15, f32[256]{0:T(256)S(1)} %get-tuple-element.14, f32[256]{0:T(256)S(1)} %get-tuple-element.20), kind=kLoop, calls=%fused_computation.23 | loop fusion | flops 2097152 | bytes 6294528 | tf_op jit(solution)/shard_map/add | solution.py:115
  (118 shorter events, 64.2 us)
Async XLA Ops:
  0.6 32.4 %copy-start = (f32[1,1,1,16,128,128]{5,4,3,2,1,0:T(8,128)S(1)}, f32[1,1,1,16,128,128]{5,4,3,2,1,0:T(8,128)}, u32[]{:S(2)}) copy-start(f32[1,1,1,16,128,128]{5,4,3,2,1,0:T(8,128)} %param.7) | copy-start | bytes 3145732
  4.8 12.5 %copy-start.9 = (s32[1,1,1,6,2]{3,4,2,1,0:T(2,128)S(1)}, s32[1,1,1,6,2]{3,4,2,1,0:T(2,128)}, u32[]{:S(2)}) copy-start(s32[1,1,1,6,2]{3,4,2,1,0:T(2,128)} %param.9) | copy-start | bytes 148
  6.4 11.3 %collective-permute-start = (f32[1,2,128,256]{3,2,1,0:T(8,128)S(1)}, f32[1,2,128,256]{3,2,1,0:T(8,128)S(1)}, u32[]{:S(2)}, u32[]{:S(2)}) collective-permute-start(f32[1,2,128,256]{3,2,1,0:T(8,128)S(1)} %get-tuple-element.52), channel_id=1, source_target_pairs={{8,0},{16,8},{24,16},{9,1},{17,9},{25,17},{10,2},{18,10},{26,18},{... | collective-permute-start | bytes 786440 | tf_op jit(solution)/shard_map/ppermute | solution.py:17
  7.7 14.4 %collective-permute-start.1 = (f32[1,2,128,256]{3,2,1,0:T(8,128)S(1)}, f32[1,2,128,256]{3,2,1,0:T(8,128)S(1)}, u32[]{:S(2)}, u32[]{:S(2)}) collective-permute-start(f32[1,2,128,256]{3,2,1,0:T(8,128)S(1)} %get-tuple-element.51), channel_id=1, source_target_pairs={{0,8},{8,16},{16,24},{1,9},{9,17},{17,25},{2,10},{10,18},{18,26},{... | collective-permute-start | bytes 786440 | tf_op jit(solution)/shard_map/ppermute | solution.py:16
  13.3 15.4 %collective-permute-start.5 = (f32[1,2,128,256]{3,2,1,0:T(8,128)S(1)}, f32[1,2,128,256]{3,2,1,0:T(8,128)S(1)}, u32[]{:S(2)}, u32[]{:S(2)}) collective-permute-start(f32[1,2,128,256]{3,2,1,0:T(8,128)S(1)} %get-tuple-element.47), channel_id=1, source_target_pairs={{0,1},{2,3},{4,5},{6,7},{8,9},{10,11},{12,13},{14,15},{16,17},{18,... | collective-permute-start | bytes 786440 | tf_op jit(solution)/shard_map/ppermute | solution.py:16
  14.8 13.9 %collective-permute-start.4 = (f32[1,2,128,256]{3,2,1,0:T(8,128)S(1)}, f32[1,2,128,256]{3,2,1,0:T(8,128)S(1)}, u32[]{:S(2)}, u32[]{:S(2)}) collective-permute-start(f32[1,2,128,256]{3,2,1,0:T(8,128)S(1)} %get-tuple-element.48), channel_id=1, source_target_pairs={{1,0},{3,2},{5,4},{7,6},{9,8},{11,10},{13,12},{15,14},{17,16},{19,... | collective-permute-start | bytes 786440 | tf_op jit(solution)/shard_map/ppermute | solution.py:17
  16.1 10.9 %collective-permute-start.2 = (f32[1,2,128,256]{3,2,1,0:T(8,128)S(1)}, f32[1,2,128,256]{3,2,1,0:T(8,128)S(1)}, u32[]{:S(2)}, u32[]{:S(2)}) collective-permute-start(f32[1,2,128,256]{3,2,1,0:T(8,128)S(1)} %get-tuple-element.50), channel_id=1, source_target_pairs={{2,0},{4,2},{6,4},{3,1},{5,3},{7,5},{10,8},{12,10},{14,12},{11,9},... | collective-permute-start | bytes 786440 | tf_op jit(solution)/shard_map/ppermute | solution.py:17
  17.6 11.0 %collective-permute-start.3 = (f32[1,2,128,256]{3,2,1,0:T(8,128)S(1)}, f32[1,2,128,256]{3,2,1,0:T(8,128)S(1)}, u32[]{:S(2)}, u32[]{:S(2)}) collective-permute-start(f32[1,2,128,256]{3,2,1,0:T(8,128)S(1)} %get-tuple-element.49), channel_id=1, source_target_pairs={{0,2},{2,4},{4,6},{1,3},{3,5},{5,7},{8,10},{10,12},{12,14},{9,11},... | collective-permute-start | bytes 786440 | tf_op jit(solution)/shard_map/ppermute | solution.py:16
  28.7 1.1 copy-start.2
  44.3 13.6 %collective-permute-start.6 = (f32[1,2,128,256]{2,3,1,0:T(8,128)}, f32[1,2,128,256]{2,3,1,0:T(8,128)}, u32[]{:S(2)}, u32[]{:S(2)}) collective-permute-start(f32[1,2,128,256]{2,3,1,0:T(8,128)} %get-tuple-element.46), channel_id=1, source_target_pairs={{8,0},{16,8},{24,16},{9,1},{17,9},{25,17},{10,2},{18,10},{26,18},{... | collective-permute-start | bytes 786440 | tf_op jit(solution)/shard_map/ppermute | solution.py:17
  45.6 20.5 %collective-permute-start.7 = (f32[1,2,128,256]{2,3,1,0:T(8,128)}, f32[1,2,128,256]{2,3,1,0:T(8,128)}, u32[]{:S(2)}, u32[]{:S(2)}) collective-permute-start(f32[1,2,128,256]{2,3,1,0:T(8,128)} %get-tuple-element.45), channel_id=1, source_target_pairs={{0,8},{8,16},{16,24},{1,9},{9,17},{17,25},{2,10},{10,18},{18,26},{... | collective-permute-start | bytes 786440 | tf_op jit(solution)/shard_map/ppermute | solution.py:16
  50.9 17.0 %collective-permute-start.8 = (f32[1,2,128,256]{2,3,1,0:T(8,128)}, f32[1,2,128,256]{2,3,1,0:T(8,128)}, u32[]{:S(2)}, u32[]{:S(2)}) collective-permute-start(f32[1,2,128,256]{2,3,1,0:T(8,128)} %get-tuple-element.44), channel_id=1, source_target_pairs={{2,0},{4,2},{6,4},{3,1},{5,3},{7,5},{10,8},{12,10},{14,12},{11,9},... | collective-permute-start | bytes 786440 | tf_op jit(solution)/shard_map/ppermute | solution.py:17
  55.2 17.4 %collective-permute-start.11 = (f32[1,2,128,256]{2,3,1,0:T(8,128)S(1)}, f32[1,2,128,256]{2,3,1,0:T(8,128)S(1)}, u32[]{:S(2)}, u32[]{:S(2)}) collective-permute-start(f32[1,2,128,256]{2,3,1,0:T(8,128)S(1)} %get-tuple-element.41), channel_id=1, source_target_pairs={{0,1},{2,3},{4,5},{6,7},{8,9},{10,11},{12,13},{14,15},{16,17},{18,... | collective-permute-start | bytes 786440 | tf_op jit(solution)/shard_map/ppermute | solution.py:16
  56.6 15.2 %collective-permute-start.10 = (f32[1,2,128,256]{2,3,1,0:T(8,128)}, f32[1,2,128,256]{2,3,1,0:T(8,128)S(1)}, u32[]{:S(2)}, u32[]{:S(2)}) collective-permute-start(f32[1,2,128,256]{2,3,1,0:T(8,128)} %get-tuple-element.42), channel_id=1, source_target_pairs={{1,0},{3,2},{5,4},{7,6},{9,8},{11,10},{13,12},{15,14},{17,16},{19,... | collective-permute-start | bytes 786440 | tf_op jit(solution)/shard_map/ppermute | solution.py:17
  57.9 13.2 %collective-permute-start.9 = (f32[1,2,128,256]{2,3,1,0:T(8,128)}, f32[1,2,128,256]{2,3,1,0:T(8,128)S(1)}, u32[]{:S(2)}, u32[]{:S(2)}) collective-permute-start(f32[1,2,128,256]{2,3,1,0:T(8,128)} %get-tuple-element.43), channel_id=1, source_target_pairs={{0,2},{2,4},{4,6},{1,3},{3,5},{5,7},{8,10},{10,12},{12,14},{9,11},... | collective-permute-start | bytes 786440 | tf_op jit(solution)/shard_map/ppermute | solution.py:16
  84.4 2.9 copy-start.10
  106.4 10.3 %collective-permute-start.12 = (f32[1,2,128,256]{3,2,1,0:T(8,128)S(1)}, f32[1,2,128,256]{3,2,1,0:T(8,128)S(1)}, u32[]{:S(2)}, u32[]{:S(2)}) collective-permute-start(f32[1,2,128,256]{3,2,1,0:T(8,128)S(1)} %get-tuple-element.40), channel_id=1, source_target_pairs={{8,0},{16,8},{24,16},{9,1},{17,9},{25,17},{10,2},{18,10},{26,18},{... | collective-permute-start | bytes 786440 | tf_op jit(solution)/shard_map/ppermute | solution.py:17
  107.7 15.3 %collective-permute-start.13 = (f32[1,2,128,256]{3,2,1,0:T(8,128)S(1)}, f32[1,2,128,256]{3,2,1,0:T(8,128)S(1)}, u32[]{:S(2)}, u32[]{:S(2)}) collective-permute-start(f32[1,2,128,256]{3,2,1,0:T(8,128)S(1)} %get-tuple-element.39), channel_id=1, source_target_pairs={{0,8},{8,16},{16,24},{1,9},{9,17},{17,25},{2,10},{10,18},{18,26},{... | collective-permute-start | bytes 786440 | tf_op jit(solution)/shard_map/ppermute | solution.py:16
  112.2 11.4 %collective-permute-start.14 = (f32[1,2,128,256]{3,2,1,0:T(8,128)S(1)}, f32[1,2,128,256]{3,2,1,0:T(8,128)S(1)}, u32[]{:S(2)}, u32[]{:S(2)}) collective-permute-start(f32[1,2,128,256]{3,2,1,0:T(8,128)S(1)} %get-tuple-element.38), channel_id=1, source_target_pairs={{2,0},{4,2},{6,4},{3,1},{5,3},{7,5},{10,8},{12,10},{14,12},{11,9},... | collective-permute-start | bytes 786440 | tf_op jit(solution)/shard_map/ppermute | solution.py:17
  113.5 16.7 %collective-permute-start.17 = (f32[1,2,128,256]{3,2,1,0:T(8,128)S(1)}, f32[1,2,128,256]{3,2,1,0:T(8,128)S(1)}, u32[]{:S(2)}, u32[]{:S(2)}) collective-permute-start(f32[1,2,128,256]{3,2,1,0:T(8,128)S(1)} %get-tuple-element.35), channel_id=1, source_target_pairs={{0,1},{2,3},{4,5},{6,7},{8,9},{10,11},{12,13},{14,15},{16,17},{18,... | collective-permute-start | bytes 786440 | tf_op jit(solution)/shard_map/ppermute | solution.py:16
  115.2 14.3 %collective-permute-start.16 = (f32[1,2,128,256]{3,2,1,0:T(8,128)S(1)}, f32[1,2,128,256]{3,2,1,0:T(8,128)S(1)}, u32[]{:S(2)}, u32[]{:S(2)}) collective-permute-start(f32[1,2,128,256]{3,2,1,0:T(8,128)S(1)} %get-tuple-element.36), channel_id=1, source_target_pairs={{1,0},{3,2},{5,4},{7,6},{9,8},{11,10},{13,12},{15,14},{17,16},{19,... | collective-permute-start | bytes 786440 | tf_op jit(solution)/shard_map/ppermute | solution.py:17
  116.7 12.0 %collective-permute-start.15 = (f32[1,2,128,256]{3,2,1,0:T(8,128)S(1)}, f32[1,2,128,256]{3,2,1,0:T(8,128)S(1)}, u32[]{:S(2)}, u32[]{:S(2)}) collective-permute-start(f32[1,2,128,256]{3,2,1,0:T(8,128)S(1)} %get-tuple-element.37), channel_id=1, source_target_pairs={{0,2},{2,4},{4,6},{1,3},{3,5},{5,7},{8,10},{10,12},{12,14},{9,11},... | collective-permute-start | bytes 786440 | tf_op jit(solution)/shard_map/ppermute | solution.py:16
  181.7 5.7 %copy-start.7 = (f32[256]{0:T(256)}, f32[256]{0:T(256)S(1)}, u32[]{:S(2)}) copy-start(f32[256]{0:T(256)S(1)} %get-tuple-element.11) | copy-start | bytes 3076
  181.7 5.7 %copy-start.3 = (f32[256]{0:T(256)}, f32[256]{0:T(256)S(1)}, u32[]{:S(2)}) copy-start(f32[256]{0:T(256)S(1)} %get-tuple-element.18) | copy-start | bytes 3076
  181.7 5.7 %copy-start.5 = (f32[256]{0:T(256)}, f32[256]{0:T(256)S(1)}, u32[]{:S(2)}) copy-start(f32[256]{0:T(256)S(1)} %get-tuple-element.19) | copy-start | bytes 3076
  194.6 13.5 %collective-permute-start.18 = (f32[1,2,128,256]{2,3,1,0:T(8,128)}, f32[1,2,128,256]{2,3,1,0:T(8,128)}, u32[]{:S(2)}, u32[]{:S(2)}) collective-permute-start(f32[1,2,128,256]{2,3,1,0:T(8,128)} %get-tuple-element.34), channel_id=1, source_target_pairs={{8,0},{16,8},{24,16},{9,1},{17,9},{25,17},{10,2},{18,10},{26,18},{... | collective-permute-start | bytes 786440 | tf_op jit(solution)/shard_map/ppermute | solution.py:17
  195.9 18.7 %collective-permute-start.19 = (f32[1,2,128,256]{2,3,1,0:T(8,128)S(1)}, f32[1,2,128,256]{2,3,1,0:T(8,128)}, u32[]{:S(2)}, u32[]{:S(2)}) collective-permute-start(f32[1,2,128,256]{2,3,1,0:T(8,128)S(1)} %get-tuple-element.33), channel_id=1, source_target_pairs={{0,8},{8,16},{16,24},{1,9},{9,17},{17,25},{2,10},{10,18},{18,26},{... | collective-permute-start | bytes 786440 | tf_op jit(solution)/shard_map/ppermute | solution.py:16
  201.2 15.1 %collective-permute-start.20 = (f32[1,2,128,256]{2,3,1,0:T(8,128)S(1)}, f32[1,2,128,256]{2,3,1,0:T(8,128)}, u32[]{:S(2)}, u32[]{:S(2)}) collective-permute-start(f32[1,2,128,256]{2,3,1,0:T(8,128)S(1)} %get-tuple-element.32), channel_id=1, source_target_pairs={{2,0},{4,2},{6,4},{3,1},{5,3},{7,5},{10,8},{12,10},{14,12},{11,9},... | collective-permute-start | bytes 786440 | tf_op jit(solution)/shard_map/ppermute | solution.py:17
  205.5 15.4 %collective-permute-start.23 = (f32[1,2,128,256]{2,3,1,0:T(8,128)S(1)}, f32[1,2,128,256]{2,3,1,0:T(8,128)S(1)}, u32[]{:S(2)}, u32[]{:S(2)}) collective-permute-start(f32[1,2,128,256]{2,3,1,0:T(8,128)S(1)} %get-tuple-element.29), channel_id=1, source_target_pairs={{0,1},{2,3},{4,5},{6,7},{8,9},{10,11},{12,13},{14,15},{16,17},{18,... | collective-permute-start | bytes 786440 | tf_op jit(solution)/shard_map/ppermute | solution.py:16
  206.8 13.4 %collective-permute-start.22 = (f32[1,2,128,256]{2,3,1,0:T(8,128)S(1)}, f32[1,2,128,256]{2,3,1,0:T(8,128)S(1)}, u32[]{:S(2)}, u32[]{:S(2)}) collective-permute-start(f32[1,2,128,256]{2,3,1,0:T(8,128)S(1)} %get-tuple-element.30), channel_id=1, source_target_pairs={{1,0},{3,2},{5,4},{7,6},{9,8},{11,10},{13,12},{15,14},{17,16},{19,... | collective-permute-start | bytes 786440 | tf_op jit(solution)/shard_map/ppermute | solution.py:17
  208.1 11.3 %collective-permute-start.21 = (f32[1,2,128,256]{2,3,1,0:T(8,128)S(1)}, f32[1,2,128,256]{2,3,1,0:T(8,128)S(1)}, u32[]{:S(2)}, u32[]{:S(2)}) collective-permute-start(f32[1,2,128,256]{2,3,1,0:T(8,128)S(1)} %get-tuple-element.31), channel_id=1, source_target_pairs={{0,2},{2,4},{4,6},{1,3},{3,5},{5,7},{8,10},{10,12},{12,14},{9,11},... | collective-permute-start | bytes 786440 | tf_op jit(solution)/shard_map/ppermute | solution.py:16
  232.5 2.9 copy-start.11
  254.2 10.3 %collective-permute-start.24 = (f32[1,2,128,256]{3,2,1,0:T(8,128)S(1)}, f32[1,2,128,256]{3,2,1,0:T(8,128)S(1)}, u32[]{:S(2)}, u32[]{:S(2)}) collective-permute-start(f32[1,2,128,256]{3,2,1,0:T(8,128)S(1)} %get-tuple-element.28), channel_id=1, source_target_pairs={{8,0},{16,8},{24,16},{9,1},{17,9},{25,17},{10,2},{18,10},{26,18},{... | collective-permute-start | bytes 786440 | tf_op jit(solution)/shard_map/ppermute | solution.py:17
  255.5 15.3 %collective-permute-start.25 = (f32[1,2,128,256]{3,2,1,0:T(8,128)S(1)}, f32[1,2,128,256]{3,2,1,0:T(8,128)S(1)}, u32[]{:S(2)}, u32[]{:S(2)}) collective-permute-start(f32[1,2,128,256]{3,2,1,0:T(8,128)S(1)} %get-tuple-element.27), channel_id=1, source_target_pairs={{0,8},{8,16},{16,24},{1,9},{9,17},{17,25},{2,10},{10,18},{18,26},{... | collective-permute-start | bytes 786440 | tf_op jit(solution)/shard_map/ppermute | solution.py:16
  260.1 11.4 %collective-permute-start.26 = (f32[1,2,128,256]{3,2,1,0:T(8,128)S(1)}, f32[1,2,128,256]{3,2,1,0:T(8,128)S(1)}, u32[]{:S(2)}, u32[]{:S(2)}) collective-permute-start(f32[1,2,128,256]{3,2,1,0:T(8,128)S(1)} %get-tuple-element.26), channel_id=1, source_target_pairs={{2,0},{4,2},{6,4},{3,1},{5,3},{7,5},{10,8},{12,10},{14,12},{11,9},... | collective-permute-start | bytes 786440 | tf_op jit(solution)/shard_map/ppermute | solution.py:17
  261.4 16.3 %collective-permute-start.29 = (f32[1,2,128,256]{3,2,1,0:T(8,128)S(1)}, f32[1,2,128,256]{3,2,1,0:T(8,128)S(1)}, u32[]{:S(2)}, u32[]{:S(2)}) collective-permute-start(f32[1,2,128,256]{3,2,1,0:T(8,128)S(1)} %get-tuple-element.23), channel_id=1, source_target_pairs={{0,1},{2,3},{4,5},{6,7},{8,9},{10,11},{12,13},{14,15},{16,17},{18,... | collective-permute-start | bytes 786440 | tf_op jit(solution)/shard_map/ppermute | solution.py:16
  263.0 14.0 %collective-permute-start.28 = (f32[1,2,128,256]{3,2,1,0:T(8,128)S(1)}, f32[1,2,128,256]{3,2,1,0:T(8,128)S(1)}, u32[]{:S(2)}, u32[]{:S(2)}) collective-permute-start(f32[1,2,128,256]{3,2,1,0:T(8,128)S(1)} %get-tuple-element.24), channel_id=1, source_target_pairs={{1,0},{3,2},{5,4},{7,6},{9,8},{11,10},{13,12},{15,14},{17,16},{19,... | collective-permute-start | bytes 786440 | tf_op jit(solution)/shard_map/ppermute | solution.py:17
  264.5 11.7 %collective-permute-start.27 = (f32[1,2,128,256]{3,2,1,0:T(8,128)S(1)}, f32[1,2,128,256]{3,2,1,0:T(8,128)S(1)}, u32[]{:S(2)}, u32[]{:S(2)}) collective-permute-start(f32[1,2,128,256]{3,2,1,0:T(8,128)S(1)} %get-tuple-element.25), channel_id=1, source_target_pairs={{0,2},{2,4},{4,6},{1,3},{3,5},{5,7},{8,10},{10,12},{12,14},{9,11},... | collective-permute-start | bytes 786440 | tf_op jit(solution)/shard_map/ppermute | solution.py:16
  278.4 4.5 %copy-start.4 = (f32[256]{0:T(256)S(1)}, f32[256]{0:T(256)}, u32[]{:S(2)}) copy-start(f32[256]{0:T(256)} %copy-done.3) | copy-start | bytes 3076
  278.5 4.5 %copy-start.6 = (f32[256]{0:T(256)S(1)}, f32[256]{0:T(256)}, u32[]{:S(2)}) copy-start(f32[256]{0:T(256)} %copy-done.5) | copy-start | bytes 3076
  282.9 45.3 %copy-start.8 = (f32[256]{0:T(256)S(1)}, f32[256]{0:T(256)}, u32[]{:S(2)}) copy-start(f32[256]{0:T(256)} %copy-done.7) | copy-start | bytes 3076
  328.9 4.0 %copy-start.1 = (f32[1,1,1,16,128,128]{5,4,3,2,1,0:T(8,128)S(1)}, f32[1,1,1,16,128,128]{5,4,3,2,1,0:T(8,128)}, u32[]{:S(2)}) copy-start(f32[1,1,1,16,128,128]{5,4,3,2,1,0:T(8,128)} %param.7) | copy-start | bytes 3145732
where the time goes:
time: 335 us; the launch traced here: 333 us
  blocking collectives  86 us (26%)
  local copies, waits for them, and re-layouts  83.5 us (25%)
  starting transfers between devices  78.7 us (23%)
  other arithmetic  39.6 us (12%)
  matrix products  25.2 us (8%)
  waiting for transfers between devices  18.6 us (6%)
    ppermute x15, starting transfers between devices, extended_2(): before = lax.ppermute(last, axis, up)  59.4 us
    psum x1, blocking collectives, on_device(): lax.psum((partial_product(assembled_load, assembled_load), partial_produc...  44 us
    psum x1, blocking collectives, on_device(): lax.psum((partial_product(working, basis_first), partial_product(working,...  42 us
    unnamed x50, local copies, waits for them, and re-layouts  22.4 us
    scatter-add x5, other arithmetic, assemble(): extended.at[slot_flat]  21 us
    ppermute x15, starting transfers between devices, extended_2(): after = lax.ppermute(leading, axis, down)  19.3 us
    dot_general x2, matrix products, operate(): product = jnp.dot(matrix, narrow, preferred_element_type=jnp.float32)  15.7 us
    concatenate x6, local copies, waits for them, and re-layouts, assemble(): jnp.concatenate([blocks, jnp.zeros((1, block_rows, row_width), jnp.float3...  15.7 us
  transfers between devices with their start and end apart: 30, of which 9 were waited for; matrix products, arithmetic and copies ran while one was open for 8% of the time, Pallas kernels for 0%

commit v1 on v0

--- a/solution.py
+++ b/solution.py
@@ -70,13 +70,19 @@
 
     precond_raw = precondition(assembled_load)
     working_raw = operate(precond_raw)
-    load_square, cross_first, raw_square = lax.psum(
+
+    def put_lines(array_here, net_axis, mesh_dim="gx"):
+        for dev_j in (net_axis, mesh_dim):
+            array_here = jax.lax.psum(array_here, dev_j)
+        return array_here
+
+    load_square, cross_first, raw_square = put_lines(
         (
             partial_product(assembled_load, assembled_load),
             partial_product(working_raw, assembled_load),
             partial_product(working_raw, working_raw),
         ),
-        ("gx", "gy", "gz"),
+        ("gy", "gz"),
     )
     initial = jnp.sqrt(load_square + epsilon)
     rescale = 1.0 / initial

time: 335 us -> 316 us (0.943)
  blocking collectives: 86 us -> 67.8 us
    psum x1 -> x2, blocking collectives: 44 us -> 27.1 us  [put_lines(): array_here = jax.lax.psum(array_here, dev_j)]
where the time goes in v1:
time: 316 us; the launch traced here: 314 us
  local copies, waits for them, and re-layouts  83.5 us (26%)
  starting transfers between devices  78 us (25%)
  blocking collectives  67.8 us (21%)
  other arithmetic  39.6 us (13%)
  matrix products  25.2 us (8%)
  waiting for transfers between devices  18.9 us (6%)
    ppermute x15, starting transfers between devices, extended_2(): before = lax.ppermute(last, axis, up)  58.4 us
    psum x1, blocking collectives, on_device(): lax.psum((partial_product(working, basis_first), partial_product(working,...  40.7 us
    psum x2, blocking collectives, put_lines(): array_here = jax.lax.psum(array_here, dev_j)  27.1 us
    unnamed x50, local copies, waits for them, and re-layouts  22.3 us
    scatter-add x5, other arithmetic, assemble(): extended.at[slot_flat]  21 us
    ppermute x15, starting transfers between devices, extended_2(): after = lax.ppermute(leading, axis, down)  19.6 us
    concatenate x6, local copies, waits for them, and re-layouts, assemble(): jnp.concatenate([blocks, jnp.zeros((1, block_rows, row_width), jnp.float3...  15.7 us
    dot_general x2, matrix products, operate(): product = jnp.dot(matrix, narrow, preferred_element_type=jnp.float32)  15.7 us
  transfers between devices with their start and end apart: 30, of which 9 were waited for; matrix products, arithmetic and copies ran while one was open for 8% of the time, Pallas kernels for 0%

profile of v1, /device:TPU:0, one launch (start us, length us, event | category | flops | bytes accessed | tf_op | source)
XLA Modules:
  0.0 314.0 jit_solution(14527493924536510107)
XLA Ops:
  3.1 1.8 gather_fusion
  7.7 5.6 %collective-permute-start.1 = (f32[1,2,128,256]{3,2,1,0:T(8,128)S(1)}, f32[1,2,128,256]{3,2,1,0:T(8,128)S(1)}, u32[]{:S(2)}, u32[]{:S(2)}) collective-permute-start(f32[1,2,128,256]{3,2,1,0:T(8,128)S(1)} %get-tuple-element.54), channel_id=1, source_target_pairs={{0,8},{8,16},{16,24},{1,9},{9,17},{17,25},{2,10},{10,18},{18,26},{... | collective-permute-start | bytes 786440 | tf_op jit(solution)/shard_map/ppermute | solution.py:16
  17.6 4.4 %collective-permute-start.3 = (f32[1,2,128,256]{3,2,1,0:T(8,128)S(1)}, f32[1,2,128,256]{3,2,1,0:T(8,128)S(1)}, u32[]{:S(2)}, u32[]{:S(2)}) collective-permute-start(f32[1,2,128,256]{3,2,1,0:T(8,128)S(1)} %get-tuple-element.52), channel_id=1, source_target_pairs={{0,2},{2,4},{4,6},{1,3},{3,5},{5,7},{8,10},{10,12},{12,14},{9,11},... | collective-permute-start | bytes 786440 | tf_op jit(solution)/shard_map/ppermute | solution.py:16
  22.1 4.8 %collective-permute-done.2 = f32[1,2,128,256]{3,2,1,0:T(8,128)S(1)} collective-permute-done((f32[1,2,128,256]{3,2,1,0:T(8,128)S(1)}, f32[1,2,128,256]{3,2,1,0:T(8,128)S(1)}, u32[]{:S(2)}, u32[]{:S(2)}) %collective-permute-start.2) | collective-permute-done | bytes 262176 | tf_op jit(solution)/shard_map/ppermute | solution.py:17
  29.9 3.1 scatter_fusion
  33.0 3.8 %convolution_bitcast_fusion.1 = f32[16,128,256]{1,2,0:T(8,128)S(1)} fusion(f32[17,128,256]{2,1,0:T(8,128)S(1)} %scatter_fusion, f32[1,1,1,16,128,128]{5,4,3,2,1,0:T(8,128)S(1)} %copy-done, f32[16]{0:T(128)S(1)} %convert_element_type.24), kind=kOutput, calls=%fused_computation.32 | convolution fusion | flops 805830656 | bytes 5243392 | tf_op jit(solution)/shard_map/bij,bjr->bir/dot_general | solution.py:57
  38.5 3.4 %gather_fusion.1 = f32[12,128,256]{1,2,0:T(8,128)} fusion(f32[17,128,256]{1,2,0:T(8,128)} %concatenate.19, s32[1024]{0:T(1024)S(1)} %pad_clamp_fusion), kind=kCustom, calls=%fused_computation.1 | custom fusion | bytes 3145776 | tf_op jit(solution)/shard_map/gather | solution.py:27
  41.9 2.4 slice_bitcast_fusion.18
  45.6 5.3 %collective-permute-start.7 = (f32[1,2,128,256]{2,3,1,0:T(8,128)}, f32[1,2,128,256]{2,3,1,0:T(8,128)}, u32[]{:S(2)}, u32[]{:S(2)}) collective-permute-start(f32[1,2,128,256]{2,3,1,0:T(8,128)} %get-tuple-element.48), channel_id=1, source_target_pairs={{0,8},{8,16},{16,24},{1,9},{9,17},{17,25},{2,10},{10,18},{18,26},{... | collective-permute-start | bytes 786440 | tf_op jit(solution)/shard_map/ppermute | solution.py:16
  52.1 3.0 copy.23
  57.9 6.6 %collective-permute-start.9 = (f32[1,2,128,256]{2,3,1,0:T(8,128)}, f32[1,2,128,256]{2,3,1,0:T(8,128)S(1)}, u32[]{:S(2)}, u32[]{:S(2)}) collective-permute-start(f32[1,2,128,256]{2,3,1,0:T(8,128)} %get-tuple-element.46), channel_id=1, source_target_pairs={{0,2},{2,4},{4,6},{1,3},{3,5},{5,7},{8,10},{10,12},{12,14},{9,11},... | collective-permute-start | bytes 786440 | tf_op jit(solution)/shard_map/ppermute | solution.py:16
  73.3 3.0 copy.24
  76.3 4.5 %scatter_fusion.1 = f32[17,128,256]{2,1,0:T(8,128)} fusion(f32[17,128,256]{2,1,0:T(8,128)} %copy.23, s32[12]{0:T(128)S(1)} %fusion.24, f32[12,128,256]{2,1,0:T(8,128)} %copy.24), kind=kCustom, calls=%fused_computation.6 | custom fusion | flops 393216 | bytes 4718640 | tf_op jit(solution)/shard_map/scatter-add | solution.py:34
  80.7 3.6 %fusion.28 = (bf16[16,128,256]{2,1,0:T(8,128)(2,1)}, f32[16,128,256]{2,1,0:T(8,128)}) fusion(f32[16]{0:T(128)S(1)} %convert_element_type.24, f32[17,128,256]{2,1,0:T(8,128)} %scatter_fusion.1), kind=kLoop, calls=%fused_computation.126 | loop fusion | flops 1048576 | bytes 5242944 | tf_op jit(solution)/shard_map/convert_element_type | solution.py:64
  84.4 2.9 copy.25
  87.3 8.0 %fusion.13 = f32[2048,256]{0,1:T(8,128)} fusion(bf16[2048,256]{1,0:T(8,128)(2,1)} %bitcast.116, bf16[1,1,1,2048,2048]{4,3,2,1,0:T(8,128)(2,1)} %param.5, f32[2048,256]{0,1:T(8,128)} %copy.25, f32[2048]{0:T(1024)S(1)} %bitcast.119), kind=kOutput, calls=%fused_computation.17 | convolution fusion | flops 2148532224 | bytes 13639680 | tf_op jit(solution)/shard_map/dot_general | solution.py:65
  95.3 2.9 copy.26
  98.2 3.2 %concatenate.20 = f32[17,128,256]{2,1,0:T(8,128)} pad(f32[16,128,256]{2,1,0:T(8,128)} %bitcast.112, f32[]{:T(128)} %constant.4.clone.1), padding=0_1x0_0x0_0 | pad | bytes 4325380 | tf_op jit(solution)/shard_map/concatenate | solution.py:25
  101.4 3.4 %gather_fusion.2 = f32[12,128,256]{2,1,0:T(8,128)} fusion(f32[17,128,256]{2,1,0:T(8,128)} %concatenate.20, s32[1024]{0:T(1024)S(1)} %pad_clamp_fusion), kind=kCustom, calls=%fused_computation.2 | custom fusion | bytes 3145776 | tf_op jit(solution)/shard_map/gather | solution.py:27
  107.6 4.6 %collective-permute-start.13 = (f32[1,2,128,256]{3,2,1,0:T(8,128)S(1)}, f32[1,2,128,256]{3,2,1,0:T(8,128)S(1)}, u32[]{:S(2)}, u32[]{:S(2)}) collective-permute-start(f32[1,2,128,256]{3,2,1,0:T(8,128)S(1)} %get-tuple-element.42), channel_id=1, source_target_pairs={{0,8},{8,16},{16,24},{1,9},{9,17},{17,25},{2,10},{10,18},{18,26},{... | collective-permute-start | bytes 786440 | tf_op jit(solution)/shard_map/ppermute | solution.py:16
  116.8 5.4 %collective-permute-start.15 = (f32[1,2,128,256]{3,2,1,0:T(8,128)S(1)}, f32[1,2,128,256]{3,2,1,0:T(8,128)S(1)}, u32[]{:S(2)}, u32[]{:S(2)}) collective-permute-start(f32[1,2,128,256]{3,2,1,0:T(8,128)S(1)} %get-tuple-element.40), channel_id=1, source_target_pairs={{0,2},{2,4},{4,6},{1,3},{3,5},{5,7},{8,10},{10,12},{12,14},{9,11},... | collective-permute-start | bytes 786440 | tf_op jit(solution)/shard_map/ppermute | solution.py:16
  124.4 4.3 %collective-permute-done.15 = f32[1,2,128,256]{3,2,1,0:T(8,128)S(1)} collective-permute-done((f32[1,2,128,256]{3,2,1,0:T(8,128)S(1)}, f32[1,2,128,256]{3,2,1,0:T(8,128)S(1)}, u32[]{:S(2)}, u32[]{:S(2)}) %collective-permute-start.15) | collective-permute-done | bytes 262176 | tf_op jit(solution)/shard_map/ppermute | solution.py:16
  130.9 4.5 %scatter_fusion.2 = f32[17,128,256]{2,1,0:T(8,128)} fusion(f32[17,128,256]{2,1,0:T(8,128)} %concatenate.20, s32[12]{0:T(128)S(1)} %fusion.24, f32[12,128,256]{2,1,0:T(8,128)} %bitcast.31), kind=kCustom, calls=%fused_computation.7 | custom fusion | flops 393216 | bytes 4718640 | tf_op jit(solution)/shard_map/scatter-add | solution.py:34
  135.4 2.2 multiply_reduce_fusion.4
  137.7 17.0 %all-reduce.6 = (f32[256]{0:T(256)S(1)}, f32[256]{0:T(256)S(1)}, f32[256]{0:T(256)S(1)}) all-reduce(f32[256]{0:T(256)S(1)} %broadcast_multiply_fusion.5, f32[256]{0:T(256)S(1)} %get-tuple-element.57, f32[256]{0:T(256)S(1)} %get-tuple-element.58), channel_id=1, replica_groups=mesh['gx'=4,'gy'=4,'gz'=2] {'gy','gz'}, use_global_device_ids=true, to_apply=%region_3.0 | all-reduce | flops 768 | bytes 6144 | tf_op jit(solution)/shard_map/psum | solution.py:76
  154.6 10.1 %all-reduce.7 = (f32[256]{0:T(256)S(1)}, f32[256]{0:T(256)S(1)}, f32[256]{0:T(256)S(1)}) all-reduce(f32[256]{0:T(256)S(1)} %get-tuple-element.11, f32[256]{0:T(256)S(1)} %get-tuple-element.12, f32[256]{0:T(256)S(1)} %get-tuple-element.13), channel_id=1, replica_groups=mesh['gx'=4,'gy'=4,'gz'=2] {'gx'}, use_global_device_ids=true, to_apply=%region_4.0 | all-reduce | flops 768 | bytes 6144 | tf_op jit(solution)/shard_map/psum | solution.py:76
  164.8 5.7 %convolution_bitcast_fusion = f32[16,128,256]{1,2,0:T(8,128)S(1)} fusion(f32[1,1,1,16,128,128]{5,4,3,2,1,0:T(8,128)S(1)} %copy-done, f32[17,128,256]{2,1,0:T(8,128)} %scatter_fusion.2, f32[17,128,256]{2,1,0:T(8,128)S(1)} %scatter_fusion, f32[256]{0:T(256)S(1)} %get-tuple-element.21, f32[256]{0:T(256)S(1)} %get-tuple-element.22, ...), kind=kOutput, calls=%fused_computation.31 | convolution fusion | flops 808976384 | bytes 7343616 | tf_op jit(solution)/shard_map/bij,bjr->bir/dot_general | solution.py:57
  172.1 3.4 %gather_fusion.3 = f32[12,128,256]{1,2,0:T(8,128)} fusion(f32[17,128,256]{1,2,0:T(8,128)} %concatenate.21, s32[1024]{0:T(1024)S(1)} %pad_clamp_fusion), kind=kCustom, calls=%fused_computation.3 | custom fusion | bytes 3145776 | tf_op jit(solution)/shard_map/gather | solution.py:27
  175.6 2.2 slice_bitcast_fusion.6
  179.2 5.3 %collective-permute-start.19 = (f32[1,2,128,256]{2,3,1,0:T(8,128)S(1)}, f32[1,2,128,256]{2,3,1,0:T(8,128)}, u32[]{:S(2)}, u32[]{:S(2)}) collective-permute-start(f32[1,2,128,256]{2,3,1,0:T(8,128)S(1)} %get-tuple-element.36), channel_id=1, source_target_pairs={{0,8},{8,16},{16,24},{1,9},{9,17},{17,25},{2,10},{10,18},{18,26},{... | collective-permute-start | bytes 786440 | tf_op jit(solution)/shard_map/ppermute | solution.py:16
  185.8 3.0 copy.28
  191.4 4.6 %collective-permute-start.21 = (f32[1,2,128,256]{2,3,1,0:T(8,128)S(1)}, f32[1,2,128,256]{2,3,1,0:T(8,128)S(1)}, u32[]{:S(2)}, u32[]{:S(2)}) collective-permute-start(f32[1,2,128,256]{2,3,1,0:T(8,128)S(1)} %get-tuple-element.34), channel_id=1, source_target_pairs={{0,2},{2,4},{4,6},{1,3},{3,5},{5,7},{8,10},{10,12},{12,14},{9,11},... | collective-permute-start | bytes 786440 | tf_op jit(solution)/shard_map/ppermute | solution.py:16
  204.7 3.0 copy.29
  207.7 4.5 %scatter_fusion.3 = f32[17,128,256]{2,1,0:T(8,128)} fusion(f32[17,128,256]{2,1,0:T(8,128)} %copy.28, s32[12]{0:T(128)S(1)} %fusion.24, f32[12,128,256]{2,1,0:T(8,128)} %copy.29), kind=kCustom, calls=%fused_computation.8 | custom fusion | flops 393216 | bytes 4718640 | tf_op jit(solution)/shard_map/scatter-add | solution.py:34
  212.2 3.3 %fusion.27 = (bf16[16,128,256]{2,1,0:T(8,128)(2,1)S(1)}, f32[16,128,256]{2,1,0:T(8,128)}) fusion(f32[16]{0:T(128)S(1)} %convert_element_type.24, f32[17,128,256]{2,1,0:T(8,128)} %scatter_fusion.3), kind=kLoop, calls=%fused_computation.125 | loop fusion | flops 1048576 | bytes 5242944 | tf_op jit(solution)/shard_map/convert_element_type | solution.py:64
  215.5 2.9 copy.30
  218.4 7.7 %fusion.10 = f32[2048,256]{0,1:T(8,128)} fusion(bf16[2048,256]{1,0:T(8,128)(2,1)S(1)} %bitcast.117, bf16[1,1,1,2048,2048]{4,3,2,1,0:T(8,128)(2,1)} %param.5, f32[2048,256]{0,1:T(8,128)} %copy.30, f32[2048]{0:T(1024)S(1)} %bitcast.120), kind=kOutput, calls=%fused_computation.16 | convolution fusion | flops 2148532224 | bytes 13639680 | tf_op jit(solution)/shard_map/dot_general | solution.py:65
  226.1 3.0 copy.31
  229.1 3.2 %concatenate.22 = f32[17,128,256]{2,1,0:T(8,128)} pad(f32[16,128,256]{2,1,0:T(8,128)} %bitcast.111, f32[]{:T(128)} %constant.4.clone.1), padding=0_1x0_0x0_0 | pad | bytes 4325380 | tf_op jit(solution)/shard_map/concatenate | solution.py:25
  232.4 3.4 %gather_fusion.4 = f32[12,128,256]{2,1,0:T(8,128)} fusion(f32[17,128,256]{2,1,0:T(8,128)} %concatenate.22, s32[1024]{0:T(1024)S(1)} %pad_clamp_fusion), kind=kCustom, calls=%fused_computation.4 | custom fusion | bytes 3145776 | tf_op jit(solution)/shard_map/gather | solution.py:27
  238.6 4.6 %collective-permute-start.25 = (f32[1,2,128,256]{3,2,1,0:T(8,128)S(1)}, f32[1,2,128,256]{3,2,1,0:T(8,128)S(1)}, u32[]{:S(2)}, u32[]{:S(2)}) collective-permute-start(f32[1,2,128,256]{3,2,1,0:T(8,128)S(1)} %get-tuple-element.30), channel_id=1, source_target_pairs={{0,8},{8,16},{16,24},{1,9},{9,17},{17,25},{2,10},{10,18},{18,26},{... | collective-permute-start | bytes 786440 | tf_op jit(solution)/shard_map/ppermute | solution.py:16
  244.4 1.7 collective-permute-start.29
  247.7 4.5 %collective-permute-start.27 = (f32[1,2,128,256]{3,2,1,0:T(8,128)S(1)}, f32[1,2,128,256]{3,2,1,0:T(8,128)S(1)}, u32[]{:S(2)}, u32[]{:S(2)}) collective-permute-start(f32[1,2,128,256]{3,2,1,0:T(8,128)S(1)} %get-tuple-element.28), channel_id=1, source_target_pairs={{0,2},{2,4},{4,6},{1,3},{3,5},{5,7},{8,10},{10,12},{12,14},{9,11},... | collective-permute-start | bytes 786440 | tf_op jit(solution)/shard_map/ppermute | solution.py:16
  254.5 4.3 %collective-permute-done.27 = f32[1,2,128,256]{3,2,1,0:T(8,128)S(1)} collective-permute-done((f32[1,2,128,256]{3,2,1,0:T(8,128)S(1)}, f32[1,2,128,256]{3,2,1,0:T(8,128)S(1)}, u32[]{:S(2)}, u32[]{:S(2)}) %collective-permute-start.27) | collective-permute-done | bytes 262176 | tf_op jit(solution)/shard_map/ppermute | solution.py:16
  261.0 4.5 %scatter_fusion.4 = f32[17,128,256]{2,1,0:T(8,128)} fusion(f32[17,128,256]{2,1,0:T(8,128)} %concatenate.22, s32[12]{0:T(128)S(1)} %fusion.24, f32[12,128,256]{2,1,0:T(8,128)} %bitcast.50), kind=kCustom, calls=%fused_computation.9 | custom fusion | flops 393216 | bytes 4718640 | tf_op jit(solution)/shard_map/scatter-add | solution.py:34
  265.4 3.2 %multiply_reduce_fusion.2 = (f32[256]{0:T(256)S(1)}, f32[256]{0:T(256)S(1)}, f32[256]{0:T(256)S(1)}) fusion(f32[17,128,256]{2,1,0:T(8,128)} %scatter_fusion.4, f32[17,128,256]{2,1,0:T(8,128)S(1)} %scatter_fusion, f32[256]{0:T(256)S(1)} %get-tuple-element.23, f32[16]{0:T(128)S(1)} %convert_element_type.24, f32[256]{0:T(256)S(1)} %copy-done.4, ...), kind=kLoop, calls=%fused_computation.26 | loop fusion | flops 7339264 | bytes 6297664 | tf_op jit(solution)/shard_map/reduce_sum | solution.py:39
  268.7 40.7 %all-reduce.5 = (f32[256]{0:T(256)S(1)}, f32[256]{0:T(256)S(1)}, f32[256]{0:T(256)S(1)}) all-reduce(f32[256]{0:T(256)S(1)} %broadcast_multiply_fusion.1, f32[256]{0:T(256)S(1)} %broadcast_multiply_fusion, f32[256]{0:T(256)S(1)} %broadcast_multiply_fusion.2), channel_id=1, replica_groups=mesh['gx'=4,'gy'=4,'gz'=2] {'gx','gy','gz'}, use_global_device_ids=true, to_apply=%region_18.0 | all-reduce | flops 768 | bytes 6144 | tf_op jit(solution)/shard_map/psum | solution.py:99
  310.0 4.0 %multiply_add_fusion = f32[16,128,256]{2,1,0:T(8,128)} fusion(f32[16,128,256]{2,1,0:T(8,128)} %get-tuple-element.20, f32[16,128,256]{2,1,0:T(8,128)} %get-tuple-element.25, f32[256]{0:T(256)S(1)} %get-tuple-element.18, f32[256]{0:T(256)S(1)} %get-tuple-element.17, f32[256]{0:T(256)S(1)} %get-tuple-element.23), kind=kLoop, calls=%fused_computation.23 | loop fusion | flops 2097152 | bytes 6294528 | tf_op jit(solution)/shard_map/add | solution.py:121
  (119 shorter events, 66.3 us)
Async XLA Ops:
  0.6 32.4 %copy-start = (f32[1,1,1,16,128,128]{5,4,3,2,1,0:T(8,128)S(1)}, f32[1,1,1,16,128,128]{5,4,3,2,1,0:T(8,128)}, u32[]{:S(2)}) copy-start(f32[1,1,1,16,128,128]{5,4,3,2,1,0:T(8,128)} %param.7) | copy-start | bytes 3145732
  4.8 12.5 %copy-start.9 = (s32[1,1,1,6,2]{3,4,2,1,0:T(2,128)S(1)}, s32[1,1,1,6,2]{3,4,2,1,0:T(2,128)}, u32[]{:S(2)}) copy-start(s32[1,1,1,6,2]{3,4,2,1,0:T(2,128)} %param.9) | copy-start | bytes 148
  6.4 11.3 %collective-permute-start = (f32[1,2,128,256]{3,2,1,0:T(8,128)S(1)}, f32[1,2,128,256]{3,2,1,0:T(8,128)S(1)}, u32[]{:S(2)}, u32[]{:S(2)}) collective-permute-start(f32[1,2,128,256]{3,2,1,0:T(8,128)S(1)} %get-tuple-element.55), channel_id=1, source_target_pairs={{8,0},{16,8},{24,16},{9,1},{17,9},{25,17},{10,2},{18,10},{26,18},{... | collective-permute-start | bytes 786440 | tf_op jit(solution)/shard_map/ppermute | solution.py:17
  7.7 14.4 %collective-permute-start.1 = (f32[1,2,128,256]{3,2,1,0:T(8,128)S(1)}, f32[1,2,128,256]{3,2,1,0:T(8,128)S(1)}, u32[]{:S(2)}, u32[]{:S(2)}) collective-permute-start(f32[1,2,128,256]{3,2,1,0:T(8,128)S(1)} %get-tuple-element.54), channel_id=1, source_target_pairs={{0,8},{8,16},{16,24},{1,9},{9,17},{17,25},{2,10},{10,18},{18,26},{... | collective-permute-start | bytes 786440 | tf_op jit(solution)/shard_map/ppermute | solution.py:16
  13.3 15.4 %collective-permute-start.5 = (f32[1,2,128,256]{3,2,1,0:T(8,128)S(1)}, f32[1,2,128,256]{3,2,1,0:T(8,128)S(1)}, u32[]{:S(2)}, u32[]{:S(2)}) collective-permute-start(f32[1,2,128,256]{3,2,1,0:T(8,128)S(1)} %get-tuple-element.50), channel_id=1, source_target_pairs={{0,1},{2,3},{4,5},{6,7},{8,9},{10,11},{12,13},{14,15},{16,17},{18,... | collective-permute-start | bytes 786440 | tf_op jit(solution)/shard_map/ppermute | solution.py:16
  14.8 13.9 %collective-permute-start.4 = (f32[1,2,128,256]{3,2,1,0:T(8,128)S(1)}, f32[1,2,128,256]{3,2,1,0:T(8,128)S(1)}, u32[]{:S(2)}, u32[]{:S(2)}) collective-permute-start(f32[1,2,128,256]{3,2,1,0:T(8,128)S(1)} %get-tuple-element.51), channel_id=1, source_target_pairs={{1,0},{3,2},{5,4},{7,6},{9,8},{11,10},{13,12},{15,14},{17,16},{19,... | collective-permute-start | bytes 786440 | tf_op jit(solution)/shard_map/ppermute | solution.py:17
  16.1 10.9 %collective-permute-start.2 = (f32[1,2,128,256]{3,2,1,0:T(8,128)S(1)}, f32[1,2,128,256]{3,2,1,0:T(8,128)S(1)}, u32[]{:S(2)}, u32[]{:S(2)}) collective-permute-start(f32[1,2,128,256]{3,2,1,0:T(8,128)S(1)} %get-tuple-element.53), channel_id=1, source_target_pairs={{2,0},{4,2},{6,4},{3,1},{5,3},{7,5},{10,8},{12,10},{14,12},{11,9},... | collective-permute-start | bytes 786440 | tf_op jit(solution)/shard_map/ppermute | solution.py:17
  17.6 11.0 %collective-permute-start.3 = (f32[1,2,128,256]{3,2,1,0:T(8,128)S(1)}, f32[1,2,128,256]{3,2,1,0:T(8,128)S(1)}, u32[]{:S(2)}, u32[]{:S(2)}) collective-permute-start(f32[1,2,128,256]{3,2,1,0:T(8,128)S(1)} %get-tuple-element.52), channel_id=1, source_target_pairs={{0,2},{2,4},{4,6},{1,3},{3,5},{5,7},{8,10},{10,12},{12,14},{9,11},... | collective-permute-start | bytes 786440 | tf_op jit(solution)/shard_map/ppermute | solution.py:16
  28.7 1.1 copy-start.2
  44.3 13.6 %collective-permute-start.6 = (f32[1,2,128,256]{2,3,1,0:T(8,128)}, f32[1,2,128,256]{2,3,1,0:T(8,128)}, u32[]{:S(2)}, u32[]{:S(2)}) collective-permute-start(f32[1,2,128,256]{2,3,1,0:T(8,128)} %get-tuple-element.49), channel_id=1, source_target_pairs={{8,0},{16,8},{24,16},{9,1},{17,9},{25,17},{10,2},{18,10},{26,18},{... | collective-permute-start | bytes 786440 | tf_op jit(solution)/shard_map/ppermute | solution.py:17
  45.6 20.5 %collective-permute-start.7 = (f32[1,2,128,256]{2,3,1,0:T(8,128)}, f32[1,2,128,256]{2,3,1,0:T(8,128)}, u32[]{:S(2)}, u32[]{:S(2)}) collective-permute-start(f32[1,2,128,256]{2,3,1,0:T(8,128)} %get-tuple-element.48), channel_id=1, source_target_pairs={{0,8},{8,16},{16,24},{1,9},{9,17},{17,25},{2,10},{10,18},{18,26},{... | collective-permute-start | bytes 786440 | tf_op jit(solution)/shard_map/ppermute | solution.py:16
  50.9 17.0 %collective-permute-start.8 = (f32[1,2,128,256]{2,3,1,0:T(8,128)}, f32[1,2,128,256]{2,3,1,0:T(8,128)}, u32[]{:S(2)}, u32[]{:S(2)}) collective-permute-start(f32[1,2,128,256]{2,3,1,0:T(8,128)} %get-tuple-element.47), channel_id=1, source_target_pairs={{2,0},{4,2},{6,4},{3,1},{5,3},{7,5},{10,8},{12,10},{14,12},{11,9},... | collective-permute-start | bytes 786440 | tf_op jit(solution)/shard_map/ppermute | solution.py:17
  55.2 17.4 %collective-permute-start.11 = (f32[1,2,128,256]{2,3,1,0:T(8,128)S(1)}, f32[1,2,128,256]{2,3,1,0:T(8,128)S(1)}, u32[]{:S(2)}, u32[]{:S(2)}) collective-permute-start(f32[1,2,128,256]{2,3,1,0:T(8,128)S(1)} %get-tuple-element.44), channel_id=1, source_target_pairs={{0,1},{2,3},{4,5},{6,7},{8,9},{10,11},{12,13},{14,15},{16,17},{18,... | collective-permute-start | bytes 786440 | tf_op jit(solution)/shard_map/ppermute | solution.py:16
  56.6 15.2 %collective-permute-start.10 = (f32[1,2,128,256]{2,3,1,0:T(8,128)}, f32[1,2,128,256]{2,3,1,0:T(8,128)S(1)}, u32[]{:S(2)}, u32[]{:S(2)}) collective-permute-start(f32[1,2,128,256]{2,3,1,0:T(8,128)} %get-tuple-element.45), channel_id=1, source_target_pairs={{1,0},{3,2},{5,4},{7,6},{9,8},{11,10},{13,12},{15,14},{17,16},{19,... | collective-permute-start | bytes 786440 | tf_op jit(solution)/shard_map/ppermute | solution.py:17
  57.9 13.2 %collective-permute-start.9 = (f32[1,2,128,256]{2,3,1,0:T(8,128)}, f32[1,2,128,256]{2,3,1,0:T(8,128)S(1)}, u32[]{:S(2)}, u32[]{:S(2)}) collective-permute-start(f32[1,2,128,256]{2,3,1,0:T(8,128)} %get-tuple-element.46), channel_id=1, source_target_pairs={{0,2},{2,4},{4,6},{1,3},{3,5},{5,7},{8,10},{10,12},{12,14},{9,11},... | collective-permute-start | bytes 786440 | tf_op jit(solution)/shard_map/ppermute | solution.py:16
  84.4 2.9 copy-start.10
  106.3 10.5 %collective-permute-start.12 = (f32[1,2,128,256]{3,2,1,0:T(8,128)S(1)}, f32[1,2,128,256]{3,2,1,0:T(8,128)S(1)}, u32[]{:S(2)}, u32[]{:S(2)}) collective-permute-start(f32[1,2,128,256]{3,2,1,0:T(8,128)S(1)} %get-tuple-element.43), channel_id=1, source_target_pairs={{8,0},{16,8},{24,16},{9,1},{17,9},{25,17},{10,2},{18,10},{26,18},{... | collective-permute-start | bytes 786440 | tf_op jit(solution)/shard_map/ppermute | solution.py:17
  107.6 15.4 %collective-permute-start.13 = (f32[1,2,128,256]{3,2,1,0:T(8,128)S(1)}, f32[1,2,128,256]{3,2,1,0:T(8,128)S(1)}, u32[]{:S(2)}, u32[]{:S(2)}) collective-permute-start(f32[1,2,128,256]{3,2,1,0:T(8,128)S(1)} %get-tuple-element.42), channel_id=1, source_target_pairs={{0,8},{8,16},{16,24},{1,9},{9,17},{17,25},{2,10},{10,18},{18,26},{... | collective-permute-start | bytes 786440 | tf_op jit(solution)/shard_map/ppermute | solution.py:16
  112.2 11.5 %collective-permute-start.14 = (f32[1,2,128,256]{3,2,1,0:T(8,128)S(1)}, f32[1,2,128,256]{3,2,1,0:T(8,128)S(1)}, u32[]{:S(2)}, u32[]{:S(2)}) collective-permute-start(f32[1,2,128,256]{3,2,1,0:T(8,128)S(1)} %get-tuple-element.41), channel_id=1, source_target_pairs={{2,0},{4,2},{6,4},{3,1},{5,3},{7,5},{10,8},{12,10},{14,12},{11,9},... | collective-permute-start | bytes 786440 | tf_op jit(solution)/shard_map/ppermute | solution.py:17
  113.5 16.7 %collective-permute-start.17 = (f32[1,2,128,256]{3,2,1,0:T(8,128)S(1)}, f32[1,2,128,256]{3,2,1,0:T(8,128)S(1)}, u32[]{:S(2)}, u32[]{:S(2)}) collective-permute-start(f32[1,2,128,256]{3,2,1,0:T(8,128)S(1)} %get-tuple-element.38), channel_id=1, source_target_pairs={{0,1},{2,3},{4,5},{6,7},{8,9},{10,11},{12,13},{14,15},{16,17},{18,... | collective-permute-start | bytes 786440 | tf_op jit(solution)/shard_map/ppermute | solution.py:16
  115.2 14.2 %collective-permute-start.16 = (f32[1,2,128,256]{3,2,1,0:T(8,128)S(1)}, f32[1,2,128,256]{3,2,1,0:T(8,128)S(1)}, u32[]{:S(2)}, u32[]{:S(2)}) collective-permute-start(f32[1,2,128,256]{3,2,1,0:T(8,128)S(1)} %get-tuple-element.39), channel_id=1, source_target_pairs={{1,0},{3,2},{5,4},{7,6},{9,8},{11,10},{13,12},{15,14},{17,16},{19,... | collective-permute-start | bytes 786440 | tf_op jit(solution)/shard_map/ppermute | solution.py:17
  116.8 11.9 %collective-permute-start.15 = (f32[1,2,128,256]{3,2,1,0:T(8,128)S(1)}, f32[1,2,128,256]{3,2,1,0:T(8,128)S(1)}, u32[]{:S(2)}, u32[]{:S(2)}) collective-permute-start(f32[1,2,128,256]{3,2,1,0:T(8,128)S(1)} %get-tuple-element.40), channel_id=1, source_target_pairs={{0,2},{2,4},{4,6},{1,3},{3,5},{5,7},{8,10},{10,12},{12,14},{9,11},... | collective-permute-start | bytes 786440 | tf_op jit(solution)/shard_map/ppermute | solution.py:16
  164.7 5.7 %copy-start.7 = (f32[256]{0:T(256)}, f32[256]{0:T(256)S(1)}, u32[]{:S(2)}) copy-start(f32[256]{0:T(256)S(1)} %get-tuple-element.14) | copy-start | bytes 3076
  164.8 5.7 %copy-start.3 = (f32[256]{0:T(256)}, f32[256]{0:T(256)S(1)}, u32[]{:S(2)}) copy-start(f32[256]{0:T(256)S(1)} %get-tuple-element.21) | copy-start | bytes 3076
  164.8 5.7 %copy-start.5 = (f32[256]{0:T(256)}, f32[256]{0:T(256)S(1)}, u32[]{:S(2)}) copy-start(f32[256]{0:T(256)S(1)} %get-tuple-element.22) | copy-start | bytes 3076
  177.7 13.7 %collective-permute-start.18 = (f32[1,2,128,256]{2,3,1,0:T(8,128)}, f32[1,2,128,256]{2,3,1,0:T(8,128)}, u32[]{:S(2)}, u32[]{:S(2)}) collective-permute-start(f32[1,2,128,256]{2,3,1,0:T(8,128)} %get-tuple-element.37), channel_id=1, source_target_pairs={{8,0},{16,8},{24,16},{9,1},{17,9},{25,17},{10,2},{18,10},{26,18},{... | collective-permute-start | bytes 786440 | tf_op jit(solution)/shard_map/ppermute | solution.py:17
  179.2 18.4 %collective-permute-start.19 = (f32[1,2,128,256]{2,3,1,0:T(8,128)S(1)}, f32[1,2,128,256]{2,3,1,0:T(8,128)}, u32[]{:S(2)}, u32[]{:S(2)}) collective-permute-start(f32[1,2,128,256]{2,3,1,0:T(8,128)S(1)} %get-tuple-element.36), channel_id=1, source_target_pairs={{0,8},{8,16},{16,24},{1,9},{9,17},{17,25},{2,10},{10,18},{18,26},{... | collective-permute-start | bytes 786440 | tf_op jit(solution)/shard_map/ppermute | solution.py:16
  184.5 14.9 %collective-permute-start.20 = (f32[1,2,128,256]{2,3,1,0:T(8,128)S(1)}, f32[1,2,128,256]{2,3,1,0:T(8,128)}, u32[]{:S(2)}, u32[]{:S(2)}) collective-permute-start(f32[1,2,128,256]{2,3,1,0:T(8,128)S(1)} %get-tuple-element.35), channel_id=1, source_target_pairs={{2,0},{4,2},{6,4},{3,1},{5,3},{7,5},{10,8},{12,10},{14,12},{11,9},... | collective-permute-start | bytes 786440 | tf_op jit(solution)/shard_map/ppermute | solution.py:17
  188.8 15.2 %collective-permute-start.23 = (f32[1,2,128,256]{2,3,1,0:T(8,128)S(1)}, f32[1,2,128,256]{2,3,1,0:T(8,128)S(1)}, u32[]{:S(2)}, u32[]{:S(2)}) collective-permute-start(f32[1,2,128,256]{2,3,1,0:T(8,128)S(1)} %get-tuple-element.32), channel_id=1, source_target_pairs={{0,1},{2,3},{4,5},{6,7},{8,9},{10,11},{12,13},{14,15},{16,17},{18,... | collective-permute-start | bytes 786440 | tf_op jit(solution)/shard_map/ppermute | solution.py:16
  190.1 13.1 %collective-permute-start.22 = (f32[1,2,128,256]{2,3,1,0:T(8,128)S(1)}, f32[1,2,128,256]{2,3,1,0:T(8,128)S(1)}, u32[]{:S(2)}, u32[]{:S(2)}) collective-permute-start(f32[1,2,128,256]{2,3,1,0:T(8,128)S(1)} %get-tuple-element.33), channel_id=1, source_target_pairs={{1,0},{3,2},{5,4},{7,6},{9,8},{11,10},{13,12},{15,14},{17,16},{19,... | collective-permute-start | bytes 786440 | tf_op jit(solution)/shard_map/ppermute | solution.py:17
  191.4 11.1 %collective-permute-start.21 = (f32[1,2,128,256]{2,3,1,0:T(8,128)S(1)}, f32[1,2,128,256]{2,3,1,0:T(8,128)S(1)}, u32[]{:S(2)}, u32[]{:S(2)}) collective-permute-start(f32[1,2,128,256]{2,3,1,0:T(8,128)S(1)} %get-tuple-element.34), channel_id=1, source_target_pairs={{0,2},{2,4},{4,6},{1,3},{3,5},{5,7},{8,10},{10,12},{12,14},{9,11},... | collective-permute-start | bytes 786440 | tf_op jit(solution)/shard_map/ppermute | solution.py:16
  215.5 2.9 copy-start.11
  237.3 10.5 %collective-permute-start.24 = (f32[1,2,128,256]{3,2,1,0:T(8,128)S(1)}, f32[1,2,128,256]{3,2,1,0:T(8,128)S(1)}, u32[]{:S(2)}, u32[]{:S(2)}) collective-permute-start(f32[1,2,128,256]{3,2,1,0:T(8,128)S(1)} %get-tuple-element.31), channel_id=1, source_target_pairs={{8,0},{16,8},{24,16},{9,1},{17,9},{25,17},{10,2},{18,10},{26,18},{... | collective-permute-start | bytes 786440 | tf_op jit(solution)/shard_map/ppermute | solution.py:17
  238.6 14.5 %collective-permute-start.25 = (f32[1,2,128,256]{3,2,1,0:T(8,128)S(1)}, f32[1,2,128,256]{3,2,1,0:T(8,128)S(1)}, u32[]{:S(2)}, u32[]{:S(2)}) collective-permute-start(f32[1,2,128,256]{3,2,1,0:T(8,128)S(1)} %get-tuple-element.30), channel_id=1, source_target_pairs={{0,8},{8,16},{16,24},{1,9},{9,17},{17,25},{2,10},{10,18},{18,26},{... | collective-permute-start | bytes 786440 | tf_op jit(solution)/shard_map/ppermute | solution.py:16
  243.1 10.6 %collective-permute-start.26 = (f32[1,2,128,256]{3,2,1,0:T(8,128)S(1)}, f32[1,2,128,256]{3,2,1,0:T(8,128)S(1)}, u32[]{:S(2)}, u32[]{:S(2)}) collective-permute-start(f32[1,2,128,256]{3,2,1,0:T(8,128)S(1)} %get-tuple-element.29), channel_id=1, source_target_pairs={{2,0},{4,2},{6,4},{3,1},{5,3},{7,5},{10,8},{12,10},{14,12},{11,9},... | collective-permute-start | bytes 786440 | tf_op jit(solution)/shard_map/ppermute | solution.py:17
  244.4 15.8 %collective-permute-start.29 = (f32[1,2,128,256]{3,2,1,0:T(8,128)S(1)}, f32[1,2,128,256]{3,2,1,0:T(8,128)S(1)}, u32[]{:S(2)}, u32[]{:S(2)}) collective-permute-start(f32[1,2,128,256]{3,2,1,0:T(8,128)S(1)} %get-tuple-element.26), channel_id=1, source_target_pairs={{0,1},{2,3},{4,5},{6,7},{8,9},{10,11},{12,13},{14,15},{16,17},{18,... | collective-permute-start | bytes 786440 | tf_op jit(solution)/shard_map/ppermute | solution.py:16
  246.2 13.3 %collective-permute-start.28 = (f32[1,2,128,256]{3,2,1,0:T(8,128)S(1)}, f32[1,2,128,256]{3,2,1,0:T(8,128)S(1)}, u32[]{:S(2)}, u32[]{:S(2)}) collective-permute-start(f32[1,2,128,256]{3,2,1,0:T(8,128)S(1)} %get-tuple-element.27), channel_id=1, source_target_pairs={{1,0},{3,2},{5,4},{7,6},{9,8},{11,10},{13,12},{15,14},{17,16},{19,... | collective-permute-start | bytes 786440 | tf_op jit(solution)/shard_map/ppermute | solution.py:17
  247.7 11.0 %collective-permute-start.27 = (f32[1,2,128,256]{3,2,1,0:T(8,128)S(1)}, f32[1,2,128,256]{3,2,1,0:T(8,128)S(1)}, u32[]{:S(2)}, u32[]{:S(2)}) collective-permute-start(f32[1,2,128,256]{3,2,1,0:T(8,128)S(1)} %get-tuple-element.28), channel_id=1, source_target_pairs={{0,2},{2,4},{4,6},{1,3},{3,5},{5,7},{8,10},{10,12},{12,14},{9,11},... | collective-permute-start | bytes 786440 | tf_op jit(solution)/shard_map/ppermute | solution.py:16
  261.0 4.5 %copy-start.4 = (f32[256]{0:T(256)S(1)}, f32[256]{0:T(256)}, u32[]{:S(2)}) copy-start(f32[256]{0:T(256)} %copy-done.3) | copy-start | bytes 3076
  261.0 4.5 %copy-start.6 = (f32[256]{0:T(256)S(1)}, f32[256]{0:T(256)}, u32[]{:S(2)}) copy-start(f32[256]{0:T(256)} %copy-done.5) | copy-start | bytes 3076
  265.4 44.0 %copy-start.8 = (f32[256]{0:T(256)S(1)}, f32[256]{0:T(256)}, u32[]{:S(2)}) copy-start(f32[256]{0:T(256)} %copy-done.7) | copy-start | bytes 3076
  310.0 4.0 %copy-start.1 = (f32[1,1,1,16,128,128]{5,4,3,2,1,0:T(8,128)S(1)}, f32[1,1,1,16,128,128]{5,4,3,2,1,0:T(8,128)}, u32[]{:S(2)}) copy-start(f32[1,1,1,16,128,128]{5,4,3,2,1,0:T(8,128)} %param.7) | copy-start | bytes 3145732
